TPU v7x, 256 devices: a whole 4x4x8 slice. The times are simulated.
256 devices in a mesh: gx: 8 (over y_hi, x), gy: 8 (over z), gz: 4 (over y_lo, core).
Axes of the slice: x: 4, y: 4 (y_hi: 2, y_lo: 2; y = y_hi * 2 + y_lo), z: 8, core: 2. Of those that a mesh axis runs over, the one named last changes fastest.
Arguments:
- tokens: bfloat16 [4096, 49, 512], P(('gx', 'gy', 'gz')), may hold values from -6 to 6
- cotangent: bfloat16 [4096, 49, 512], P(('gx', 'gy', 'gz')), may hold values from -6 to 6
- regions: int32 [4096, 49], P(('gx', 'gy', 'gz')), may hold values from 0 to 3
- rel_index: int32 [49, 49], replicated, may hold values from 0 to 168
- w_qkv: bfloat16 [512, 1536], replicated, may hold values from -0.25 to 0.25
- w_proj: bfloat16 [512, 512], replicated, may hold values from -0.25 to 0.25
- bias_table: float32 [169, 16], replicated, may hold values from -4 to 4
- mom_qkv: float32 [786432], P(('gx', 'gy', 'gz')), may hold values from -0.06 to 0.06
- mom_proj: float32 [262144], P(('gx', 'gy', 'gz')), may hold values from -0.06 to 0.06
- mom_table: float32 [169, 16], replicated, may hold values from -0.06 to 0.06
Outputs:
- new_mom_qkv: float32 [786432], P(('gx', 'gy', 'gz'))
- new_mom_proj: float32 [262144], P(('gx', 'gy', 'gz'))
- new_mom_table: float32 [169, 16], replicated
All inputs are finite; a program needn't handle non-finite values.
Results may differ from a plain program's by a relative error of at most 0.015.
Values sent between devices are 32-bit elements; how exact they have to be, the bound alone decides.
A program may use at most 128 MiB of HBM per device.

v0:
```python
import functools

import jax
import jax.numpy as jnp
from jax import lax
from jax.experimental import pallas as pl
from jax.experimental.pallas import tpu as pltpu
from jax.sharding import PartitionSpec as P

MESH = pl.DeviceIdType.MESH
BF = jnp.bfloat16
F32 = jnp.float32
WIN = 16
TOK = 49
SEG = 64
TP = 56
D = 512
HEAD_DIM = 32
SCALE = HEAD_DIM ** -0.5
UNITS = 2
CH = 256
CHUNKS = 8


def nt(a, b):
    return lax.dot_general(a, b, (((1,), (1,)), ((), ())), preferred_element_type=F32)


def nn(a, b):
    return jnp.dot(a, b, preferred_element_type=F32)


def iota(shape, dim):
    return lax.broadcasted_iota(jnp.int32, shape, dim)


def onehot(condition):
    return condition.astype(F32).astype(BF)


def aligned(start, size, to=128):
    return pl.ds(pl.multiple_of(start, to), size)


def small_tables(reg, rel, tab_t, bias, mask, pad, tabp, relt):
    low = iota((TP, 128), 1) < SEG
    pad[...] = jnp.zeros_like(pad)
    pad[0:TOK, 0:TOK] = rel[...].astype(F32)
    flipped = pad[...].T
    both = flipped[0:TP] + pltpu.roll(flipped, SEG, 1)[0:TP]
    index = both.astype(jnp.int32)
    relt[...] = both
    pad[...] = jnp.zeros_like(pad)
    pad[0:WIN, 0:TOK] = reg[...].astype(F32)
    regions = pad[0:WIN, :]
    regions = regions + pltpu.roll(regions, SEG, 1)
    columns = pad[...].T[0:TP]
    for w in range(WIN):
        key = jnp.broadcast_to(columns[:, w : w + 1], (TP, 128))
        mask[w] = jnp.where(key == regions[w : w + 1], 0.0, -100.0).astype(F32)
    tabp[...] = jnp.zeros_like(tabp)
    tabp[:, 0:169] = tab_t[...]
    first = jnp.bitwise_and(index, 127)
    beyond = index >= 128
    real = iota((TP, 128), 0) < TOK

    def looked(h):
        lo = jnp.broadcast_to(tabp[h : h + 1, 0:128], (TP, 128))
        hi = jnp.broadcast_to(tabp[h : h + 1, 128:256], (TP, 128))
        lo = jnp.take_along_axis(lo, first, axis=1, mode="promise_in_bounds")
        hi = jnp.take_along_axis(hi, first, axis=1, mode="promise_in_bounds")
        return jnp.where(beyond, hi, lo)

    for k in range(8):
        value = jnp.where(low, looked(2 * k), looked(2 * k + 1))
        bias[k // 2, :, (k % 2) * 128 : (k % 2 + 1) * 128] = jnp.where(real, value, -1e30)


def gather_windows(src, dst):
    row, col = iota((256, 256), 0), iota((256, 256), 1)
    pick = onehot((row % 16) * 16 + row // 16 == col)
    for part in range(3):
        out = nn(pick, src[part * 256 : (part + 1) * 256, :]).astype(BF)
        dst[:, part * 16 : (part + 1) * 16, :] = out.reshape(WIN, 16, D)
    out = nn(pick[:, 0:16], src[768:784, :]).astype(BF)
    dst[:, 48:64, :] = out.reshape(WIN, 16, D)


def project(wqkv, wproj, xp, cp, qkv, kvt, da, xpt):
    eye = onehot(iota((128, 128), 0) == iota((128, 128), 1))
    s = iota((128, 128), 0)
    wanted = (
        (s // 32) * 32
        + ((s // 4) % 2) * 16
        + ((s // 2) % 2) * 8
        + ((s // 8) % 2) * 4
        + ((s // 16) % 2) * 2
        + s % 2
    )
    strips = onehot(wanted == iota((128, 128), 1))

    def four_windows(c, carry):
        rows = aligned(c * 256, 256, 256)
        x = xp[pl.ds(c * 4, 4)].reshape(256, D)
        y = cp[pl.ds(c * 4, 4)].reshape(256, D)
        values = nn(x, wqkv[...]).astype(BF)
        qkv[rows, :] = values
        da[rows, :] = nt(y, wproj[...]).astype(BF)
        for b in range(4):
            xpt[b * 128 : (b + 1) * 128, rows] = nt(strips, x[:, b * 128 : (b + 1) * 128]).astype(BF)
            k = values[:, 512 + b * 128 : 512 + (b + 1) * 128]
            kvt[b * 128 : (b + 1) * 128, rows] = nt(eye, k).astype(BF)
            v = values[:, 1024 + b * 128 : 1024 + (b + 1) * 128]
            kvt[512 + b * 128 : 512 + (b + 1) * 128, rows] = nt(strips, v).astype(BF)
        return carry

    lax.fori_loop(0, 4, four_windows, 0)


class Attention:
    def __init__(self, qkv, kvt, da, bias, mask, keep, dk, dv, dqt, at, gb):
        self.refs = qkv, kvt, da, bias, mask, keep, dk, dv, dqt, at, gb
        lane = iota((SEG, 256), 1) % 128
        self.heads = [onehot(lane // HEAD_DIM == h) for h in range(4)]
        self.zero = jnp.zeros((SEG, 128), BF)
        self.tail = jnp.zeros((SEG - TP, 256), F32)
        half = iota((128, 128), 1)
        self.left = onehot(half < SEG)
        self.right = onehot(half >= SEG)
        self.low = iota((32, 128), 1) < SEG

    def spread(self, a):
        a = jnp.concatenate([a[0:SEG], a[SEG:]], axis=1)
        return jnp.concatenate([a * head for head in self.heads], axis=0)

    def diagonal(self, a):
        upper = jnp.concatenate([a[0:SEG], self.zero], axis=1)
        lower = jnp.concatenate([self.zero, a[SEG:]], axis=1)
        return jnp.concatenate([upper, lower], axis=0)

    def stack(self, a, b):
        return jnp.concatenate([a, self.tail, b, self.tail], axis=0).astype(BF)

    def own(self, dst, pair, g, value):
        dst[aligned(pair * 128, SEG), aligned(g * 128, 128)] = value[0:SEG, 0:128].astype(BF)
        dst[aligned(pair * 128 + SEG, SEG, SEG), aligned(g * 128, 128)] = value[SEG:, 128:256].astype(BF)

    def across(self, dst, pair, g, turned, wide):
        lhs = jnp.concatenate([turned * self.left, turned * self.right], axis=0)
        full = nn(lhs, wide)
        for h in range(4):
            lanes = slice((h // 2) * 128, (h // 2 + 1) * 128)
            one = full[32 * h : 32 * h + 32, lanes]
            two = full[128 + 32 * h : 128 + 32 * h + 32, lanes]
            if h % 2:
                one = pltpu.roll(one, SEG, 1)
            else:
                two = pltpu.roll(two, SEG, 1)
            value = jnp.where(self.low, one, two).astype(BF)
            dst[aligned(g * 128 + 32 * h, 32, 32), aligned(pair * 128, 128)] = value

    def forward(self, g, pair):
        qkv, kvt, da, bias, mask, keep, dk, dv, dqt, at, gb = self.refs
        rows = aligned(pair * 128, 128)
        q_wide = self.spread(qkv[rows, aligned(g * 128, 128)])
        both = nt(self.diagonal(qkv[rows, aligned(512 + g * 128, 128)]), q_wide)
        probs = []
        for i in range(2):
            scores = both[i * SEG : i * SEG + TP] * SCALE + bias[g]
            scores = scores + jnp.concatenate([mask[2 * pair + i]] * 2, axis=1)
            e = jnp.exp(scores - jnp.max(scores, axis=0, keepdims=True))
            p = e * (1.0 / jnp.sum(e, axis=0, keepdims=True))
            keep[2 * pair + i, :, aligned(g * 256, 256, 256)] = p
            probs.append(p)
        probs = self.stack(*probs)
        da_wide = self.spread(da[rows, aligned(g * 128, 128)])
        self.own(dv, pair, g, nn(probs, da_wide))
        self.across(at, pair, g, kvt[aligned(512 + g * 128, 128), rows], probs)

    def backward(self, g, pair):
        qkv, kvt, da, bias, mask, keep, dk, dv, dqt, at, gb = self.refs
        rows = aligned(pair * 128, 128)
        da_wide = self.spread(da[rows, aligned(g * 128, 128)])
        both = nt(self.diagonal(qkv[rows, aligned(1024 + g * 128, 128)]), da_wide)
        parts = []
        for i in range(2):
            p = keep[2 * pair + i, :, aligned(g * 256, 256, 256)]
            dp = both[i * SEG : i * SEG + TP]
            ds = p * (dp - jnp.sum(p * dp, axis=0, keepdims=True))
            parts.append(ds)
        total = parts[0] + parts[1]
        for k in range(2):
            block = aligned((2 * g + k) * TP, TP, 8)
            gb[block, :] = gb[block, :] + total[:, k * 128 : (k + 1) * 128]
        wide = self.stack(parts[0] * SCALE, parts[1] * SCALE)
        q_wide = self.spread(qkv[rows, aligned(g * 128, 128)])
        self.own(dk, pair, g, nn(wide, q_wide))
        self.across(dqt, pair, g, kvt[aligned(g * 128, 128), rows], wide)

    def run(self, pass_, g):
        def one(t, carry):
            for u in range(UNITS):
                pass_(g, t * UNITS + u)
            return carry

        lax.fori_loop(0, WIN // 2 // UNITS, one, 0)


def table_gradient(gb, relt):
    low = iota((8, 128), 1) < SEG
    entry = iota((256, 128), 0).astype(F32)
    total = jnp.zeros((32, 256), F32)

    def line(j):
        if j >= TOK:
            return jnp.zeros((32, 128), BF), jnp.zeros((256, 128), BF)
        hot = onehot(entry == jnp.broadcast_to(relt[j : j + 1, :], (256, 128)))
        pairs = gb[pl.ds(j, 8, stride=TP), :]
        split = jnp.concatenate([jnp.where(low, pairs, 0.0), jnp.where(low, 0.0, pairs)], axis=0)
        upper = split.astype(BF)
        lower = (split - upper.astype(F32)).astype(BF)
        return jnp.concatenate([upper, lower], axis=0), hot

    for j in range(0, TOK, 2):
        a, b = line(j), line(j + 1)
        total = total + nt(
            jnp.concatenate([a[0], b[0]], axis=1), jnp.concatenate([a[1], b[1]], axis=1)
        )
    return total[0:16] + total[16:32]


class Exchange:
    def __init__(self, g, s1, ra, rb, a2, b2, ra2, rb2, zs, rz, tt, tr, send, recv):
        self.g, self.s1, self.ra, self.rb, self.a2, self.b2 = g, s1, ra, rb, a2, b2
        self.ra2, self.rb2, self.zs, self.rz, self.tt, self.tr = ra2, rb2, zs, rz, tt, tr
        self.send, self.recv, self.used = send, recv, 0
        gx, gy, gz = lax.axis_index("gx"), lax.axis_index("gy"), lax.axis_index("gz")
        x, z, core = lax.rem(gx, 4), gy, lax.rem(gz, 2)
        y = (gx // 4) * 2 + gz // 2

        def device(x, y, z, core):
            return ((y // 2) * 4 + x, z, lax.rem(y, 2) * 2 + core)

        def xor(a, b):
            out = 0
            for bit in (1, 2, 4):
                have = lax.rem(a // bit, 2)
                out = out + bit * ((1 - have) if b & bit else have)
            return out

        self.x, self.y, self.z, self.core = x, y, z, core
        self.partner = device(x, y, z, 1 - core)
        self.along_x = [(xor(x, d), device(xor(x, d), y, z, core)) for d in (1, 2, 3)]
        self.along_y = [(xor(y, d), device(x, xor(y, d), z, core)) for d in (1, 2, 3)]
        self.along_z = [(xor(z, d), device(x, y, xor(z, d), core)) for d in range(1, 8)]
        self.flight = {}

    def greet(self):
        self.peers = [self.partner] + [dev for _, dev in self.along_x + self.along_y + self.along_z]
        barrier = pltpu.get_barrier_semaphore()
        for peer in self.peers:
            pl.semaphore_signal(barrier, inc=1, device_id=peer, device_id_type=MESH)

    def greeted(self):
        pl.semaphore_wait(pltpu.get_barrier_semaphore(), len(self.peers))

    def start(self, key, src, dst, dev):
        n = self.used
        self.used += 1
        c = pltpu.make_async_remote_copy(
            src_ref=src, dst_ref=dst, send_sem=self.send.at[n], recv_sem=self.recv.at[n],
            device_id=dev, device_id_type=MESH,
        )
        c.start()
        self.flight.setdefault(key, []).append(c)

    def finish(self, key):
        for c in self.flight.pop(key):
            c.wait()

    def put(self, c, lo, value):
        lanes = slice(lo, lo + value.shape[1])
        for strip in range(16):
            y1, x, z2 = strip // 8, (strip // 2) % 4, strip % 2
            for core in range(2):
                for y0 in range(2):
                    r = strip * 32 + core * 16 + y0 * 8
                    self.g[c, core, z2, y1 * 2 + y0, x, :, lanes] = value[r : r + 8]

    def cores(self, c):
        self.start(("p0", c), self.g.at[c, 1 - self.core], self.s1.at[c], self.partner)

    def first(self, c):
        self.finish(("p0", c))
        for half in range(2):
            self.s1[c, half] = self.s1[c, half] + self.g[c, self.core, half]
        for n, (to, dev) in enumerate(self.along_x):
            self.start(("p1", c), self.s1.at[c, 0, :, to], self.ra.at[c, n], dev)
        for n, (to, dev) in enumerate(self.along_y):
            self.start(("p1", c), self.s1.at[c, 1, to], self.rb.at[c, n], dev)

    def second(self, lo, hi):
        for c in range(lo, hi):
            self.finish(("p1", c))
            self.a2[c] = self.s1[c, 0, :, self.x] + self.ra[c, 0] + self.ra[c, 1] + self.ra[c, 2]
            self.b2[c] = self.s1[c, 1, self.y] + self.rb[c, 0] + self.rb[c, 1] + self.rb[c, 2]
        span = pl.ds(lo, hi - lo)
        for n, (to, dev) in enumerate(self.along_y):
            self.start(("p2", lo), self.a2.at[span, to], self.ra2.at[n, span], dev)
        for n, (to, dev) in enumerate(self.along_x):
            self.start(("p2", lo), self.b2.at[span, to], self.rb2.at[n, span], dev)

    def third(self, lo, hi):
        self.finish(("p2", lo))
        for c in range(lo, hi):
            a = self.a2[c, self.y] + self.ra2[0, c] + self.ra2[1, c] + self.ra2[2, c]
            b = self.b2[c, self.x] + self.rb2[0, c] + self.rb2[1, c] + self.rb2[2, c]
            for k in range(4):
                self.zs[c, k] = a[2 * k : 2 * k + 2]
                self.zs[c, 4 + k] = b[2 * k : 2 * k + 2]
        span = pl.ds(lo, hi - lo)
        for n, (to, dev) in enumerate(self.along_z):
            self.start(("p3", lo), self.zs.at[span, to], self.rz.at[n, span], dev)

    def last(self, lo, hi):
        self.finish(("p3", lo))
        out = []
        for c in range(lo, hi):
            mine = self.zs[c, self.z]
            for n in range(7):
                mine = mine + self.rz[n, c]
            out.append(mine)
        return out

    def table_cores(self, value):
        self.tt[0, 0] = value[0:8]
        self.tt[0, 1] = value[8:16]
        self.start("t0", self.tt.at[0, 1 - self.core], self.tr.at[0], self.partner)

    def table_axis(self, key, stage, first, count, own, peers):
        total = own
        if key is not None:
            self.finish(key)
            for n in range(count):
                total = total + self.tr[first + n]
        self.tt[stage, 0] = total
        for n, (_, dev) in enumerate(peers):
            self.start("t%d" % stage, self.tt.at[stage, 0], self.tr.at[first + count + n], dev)


def kernel(scale, *refs):
    refs = list(refs)

    def take(n):
        out = refs[:n]
        del refs[:n]
        return out

    tok_hbm, cot_hbm, reg, rel, wqkv_hbm, wproj_hbm, tab_t = take(7)
    mom_qkv, mom_proj, mom_tab = take(3)
    out_qkv, out_proj, out_tab = take(3)
    tok, cot, wqkv, wproj, fetched = take(5)
    xp, cp, qkv, kvt, da, xpt = take(6)
    bias, mask, keep, dk, dv, dqt, at, gb, pad, tabp, relt = take(11)
    ex = Exchange(*refs)

    fetches = []
    for n, (src, dst) in enumerate(((tok_hbm, tok), (cot_hbm, cot), (wqkv_hbm, wqkv), (wproj_hbm, wproj))):
        fetch = pltpu.make_async_copy(src, dst, fetched.at[n])
        fetch.start()
        fetches.append(fetch)
    ex.greet()
    small_tables(reg, rel, tab_t, bias, mask, pad, tabp, relt)
    gb[...] = jnp.zeros_like(gb)
    fetches[0].wait()
    gather_windows(tok, xp)
    fetches[1].wait()
    gather_windows(cot, cp)
    fetches[2].wait()
    fetches[3].wait()
    project(wqkv, wproj, xp, cp, qkv, kvt, da, xpt)

    att = Attention(qkv, kvt, da, bias, mask, keep, dk, dv, dqt, at, gb)

    def v_chunk(c):
        ex.put(c, 0, nn(xpt[...], dv[:, c * 256 : (c + 1) * 256]))
        ex.cores(c)

    def proj_chunk(c):
        y = cp[:, :, c * 256 : (c + 1) * 256].reshape(WIN * SEG, 256)
        ex.put(2 + c, 0, nn(at[...], y))
        ex.cores(2 + c)

    def qk_chunk(g):
        ex.put(4 + g, 0, nt(xpt[...], dqt[g * 128 : (g + 1) * 128, :]))
        ex.put(4 + g, 128, nn(xpt[...], dk[:, g * 128 : (g + 1) * 128]))
        ex.cores(4 + g)

    att.run(att.forward, 0)
    att.run(att.forward, 1)
    ex.greeted()
    v_chunk(0)
    att.run(att.forward, 2)
    ex.first(0)
    att.run(att.forward, 3)
    v_chunk(1)
    proj_chunk(0)
    ex.first(1)
    proj_chunk(1)
    ex.first(2)
    att.run(att.backward, 0)
    ex.first(3)
    qk_chunk(0)
    att.run(att.backward, 1)
    ex.first(4)
    ex.second(0, 4)
    qk_chunk(1)
    att.run(att.backward, 2)
    ex.first(5)
    ex.third(0, 4)
    qk_chunk(2)
    att.run(att.backward, 3)
    ex.first(6)
    qk_chunk(3)
    ex.second(4, 6)
    ex.table_cores(table_gradient(gb, relt))
    ex.first(7)
    own = ex.tt[0, ex.core]
    ex.finish("t0")
    ex.table_axis(None, 1, 0, 1, own + ex.tr[0], ex.along_x)
    ex.third(4, 6)
    ex.second(6, 8)
    ex.table_axis("t1", 2, 1, 3, ex.tt[1, 0], ex.along_y)
    ex.third(6, 8)
    ex.table_axis("t2", 3, 4, 3, ex.tt[2, 0], ex.along_z)

    def finish(lo, hi):
        for c, mine in zip(range(lo, hi), ex.last(lo, hi)):
            for r in range(2):
                for part in range(2):
                    value = mine[r : r + 1, part * 128 : (part + 1) * 128] * scale
                    if 2 <= c < 4:
                        k = r * 4 + (c - 2) * 2 + part
                        out_proj[k : k + 1, :] = 0.9 * mom_proj[k : k + 1, :] + value
                    else:
                        col = 8 + c * 2 + part if c < 2 else part * 4 + c - 4
                        k = r * 12 + col
                        out_qkv[k : k + 1, :] = 0.9 * mom_qkv[k : k + 1, :] + value

    finish(0, 4)
    finish(4, 6)
    finish(6, 8)
    ex.finish("t3")
    table = ex.tt[3, 0]
    for n in range(7):
        table = table + ex.tr[7 + n]
    ex.tt[4, 0] = table
    ex.start("t4", ex.tt.at[4, 0], ex.tr.at[14], ex.partner)
    ex.finish("t4")
    core = ex.core.astype(F32)
    other = ex.tr[14]
    even = table * (1.0 - core) + other * core
    odd = table * core + other * (1.0 - core)
    for k in range(8):
        out_tab[2 * k : 2 * k + 1, :] = 0.9 * mom_tab[2 * k : 2 * k + 1, :] + even[k : k + 1, 0:169] * scale
        out_tab[2 * k + 1 : 2 * k + 2, :] = (
            0.9 * mom_tab[2 * k + 1 : 2 * k + 2, :] + odd[k : k + 1, 0:169] * scale
        )


SCRATCH = [
    pltpu.VMEM((784, D), BF),
    pltpu.VMEM((784, D), BF),
    pltpu.VMEM((D, 3 * D), BF),
    pltpu.VMEM((D, D), BF),
    pltpu.SemaphoreType.DMA((4,)),
    pltpu.VMEM((WIN, SEG, D), BF),
    pltpu.VMEM((WIN, SEG, D), BF),
    pltpu.VMEM((1024, 3 * D), BF),
    pltpu.VMEM((1024, 1024), BF),
    pltpu.VMEM((1024, D), BF),
    pltpu.VMEM((D, 1024), BF),
    pltpu.VMEM((4, TP, 256), F32),
    pltpu.VMEM((WIN, TP, 128), F32),
    pltpu.VMEM((WIN, TP, 1024), F32),
    pltpu.VMEM((1024, D), BF),
    pltpu.VMEM((1024, D), BF),
    pltpu.VMEM((D, 1024), BF),
    pltpu.VMEM((D, 1024), BF),
    pltpu.VMEM((8 * TP, 128), F32),
    pltpu.VMEM((128, 128), F32),
    pltpu.VMEM((16, 256), F32),
    pltpu.VMEM((TP, 128), F32),
    pltpu.VMEM((CHUNKS, 2, 2, 4, 4, 8, CH), F32),
    pltpu.VMEM((CHUNKS, 2, 4, 4, 8, CH), F32),
    pltpu.VMEM((CHUNKS, 3, 4, 8, CH), F32),
    pltpu.VMEM((CHUNKS, 3, 4, 8, CH), F32),
    pltpu.VMEM((CHUNKS, 4, 8, CH), F32),
    pltpu.VMEM((CHUNKS, 4, 8, CH), F32),
    pltpu.VMEM((3, CHUNKS, 8, CH), F32),
    pltpu.VMEM((3, CHUNKS, 8, CH), F32),
    pltpu.VMEM((CHUNKS, 8, 2, CH), F32),
    pltpu.VMEM((7, CHUNKS, 2, CH), F32),
    pltpu.VMEM((5, 2, 8, CH), F32),
    pltpu.VMEM((15, 8, CH), F32),
    pltpu.SemaphoreType.DMA((120,)),
    pltpu.SemaphoreType.DMA((120,)),
]


def step(scale, *operands):
    vm = pl.BlockSpec(memory_space=pltpu.VMEM)
    hbm = pl.BlockSpec(memory_space=pl.ANY)
    return pl.pallas_call(
        functools.partial(kernel, scale),
        name="step",
        out_shape=(
            jax.ShapeDtypeStruct((24, 128), F32),
            jax.ShapeDtypeStruct((8, 128), F32),
            jax.ShapeDtypeStruct((16, 169), F32),
        ),
        in_specs=[hbm, hbm, vm, vm, hbm, hbm, vm, vm, vm, vm],
        out_specs=(vm, vm, vm),
        scratch_shapes=SCRATCH,
        compiler_params=pltpu.CompilerParams(
            collective_id=0, has_side_effects=True, vmem_limit_bytes=60 * 2**20
        ),
    )(*operands)


def body(tokens, cotangent, regions, rel_index, w_qkv, w_proj, bias_table, mom_qkv, mom_proj, mom_table):
    win, count, dim = tokens.shape
    devices = lax.axis_size(("gx", "gy", "gz"))
    tok = jnp.transpose(tokens, (1, 0, 2)).reshape(count * win, dim)
    cot = jnp.transpose(cotangent, (1, 0, 2)).reshape(count * win, dim)
    out_qkv, out_proj, out_tab = step(
        1.0 / (win * devices), tok, cot, regions, rel_index, w_qkv, w_proj, bias_table.T,
        mom_qkv.reshape(24, 128), mom_proj.reshape(8, 128), mom_table.T,
    )
    return out_qkv.reshape(-1), out_proj.reshape(-1), out_tab.T


def solution(mesh):
    rows = P(("gx", "gy", "gz"))
    wide = P(("gx", "gy", "gz"), None, None)
    return jax.shard_map(
        body,
        mesh=mesh,
        in_specs=(wide, wide, P(("gx", "gy", "gz"), None), P(), P(), P(), P(), rows, rows, P()),
        out_specs=(rows, rows, P()),
        check_vma=False,
    )
```

profile of v0, /device:TPU:1, one launch (start us, length us, event | category | flops | bytes accessed | tf_op | source)
XLA Modules:
  0.0 70.5 jit_solution(782769507381874788)
XLA Ops:
  0.6 66.0 %step.1 = (f32[24,128]{1,0:T(8,128)}, f32[8,128]{1,0:T(8,128)}, f32[16,169]{1,0:T(8,128)}) custom-call(bf16[784,512]{1,0:T(8,128)(2,1)} %bitcast.13, bf16[784,512]{1,0:T(8,128)(2,1)} %bitcast.14, s32[16,49]{1,0:T(8,128)} %refs_2_.1, s32[49,49]{1,0:T(8,128)} %refs_3_.1, bf16[512,1536]{1,0:T(8,128)(2,1)} %refs_4_.1, bf16[512,512]{1,0:T(8,128)(2,1)} %refs_5_.1, ...), custom_call_target="tpu_custom_call" | custom-call | tf_op jit(solution)/shard_map/step/pallas_call | solution.py:514
  66.6 1.3 %copy.16 = f32[3072]{0:T(1024)} copy(f32[3072]{0:T(1024)} %bitcast.18) | data formatting | bytes 24576
  67.9 1.3 %copy.17 = f32[1024]{0:T(1024)} copy(f32[1024]{0:T(1024)} %bitcast.21) | data formatting | bytes 8192
  69.2 1.3 %copy.18 = f32[169,16]{0,1:T(8,128)} copy(f32[169,16]{0,1:T(8,128)} %bitcast.17) | data formatting | bytes 21632
where the time goes:
time: 70.9 us; the launch traced here: 70.5 us
  Pallas kernels  66 us (93%)
  local copies, waits for them, and re-layouts  3.9 us (6%)
    pallas_call x1, Pallas kernels, step(): pl.pallas_call(functools.partial(kernel, scale), name='step', out_shape=(...  66 us
    unnamed x3, local copies, waits for them, and re-layouts  3.9 us

commit v1 on v0

--- a/solution.py
+++ b/solution.py
@@ -17,7 +17,9 @@
 D = 512
 HEAD_DIM = 32
 SCALE = HEAD_DIM ** -0.5
-UNITS = 2
+UNITS = 4
+STEPS = 4 * WIN // 2 // UNITS
+GROUP = STEPS // 4
 CH = 256
 CHUNKS = 8
 
@@ -118,8 +120,10 @@
 
 
 class Attention:
-    def __init__(self, qkv, kvt, da, bias, mask, keep, dk, dv, dqt, at, gb):
-        self.refs = qkv, kvt, da, bias, mask, keep, dk, dv, dqt, at, gb
+    def __init__(self, qkv, kvt, da, bias, mask, keep, dk, dv, dqt, at, gb, raw, wide):
+        self.qkv, self.kvt, self.da, self.bias, self.mask = qkv, kvt, da, bias, mask
+        self.keep, self.dk, self.dv, self.dqt, self.at = keep, dk, dv, dqt, at
+        self.gb, self.raw, self.wide = gb, raw, wide
         lane = iota((SEG, 256), 1) % 128
         self.heads = [onehot(lane // HEAD_DIM == h) for h in range(4)]
         self.zero = jnp.zeros((SEG, 128), BF)
@@ -159,51 +163,82 @@
             value = jnp.where(self.low, one, two).astype(BF)
             dst[aligned(g * 128 + 32 * h, 32, 32), aligned(pair * 128, 128)] = value
 
-    def forward(self, g, pair):
-        qkv, kvt, da, bias, mask, keep, dk, dv, dqt, at, gb = self.refs
+    def place(self, unit):
+        return unit // (WIN // 2), unit % (WIN // 2)
+
+    def forward1(self, u, unit):
+        g, pair = self.place(unit)
         rows = aligned(pair * 128, 128)
-        q_wide = self.spread(qkv[rows, aligned(g * 128, 128)])
-        both = nt(self.diagonal(qkv[rows, aligned(512 + g * 128, 128)]), q_wide)
+        q_wide = self.spread(self.qkv[rows, aligned(g * 128, 128)])
+        self.raw[u] = nt(self.diagonal(self.qkv[rows, aligned(512 + g * 128, 128)]), q_wide)
+
+    def forward2(self, u, unit):
+        g, pair = self.place(unit)
         probs = []
         for i in range(2):
-            scores = both[i * SEG : i * SEG + TP] * SCALE + bias[g]
-            scores = scores + jnp.concatenate([mask[2 * pair + i]] * 2, axis=1)
+            scores = self.raw[u, i * SEG : i * SEG + TP, :] * SCALE + self.bias[g]
+            scores = scores + jnp.concatenate([self.mask[2 * pair + i]] * 2, axis=1)
             e = jnp.exp(scores - jnp.max(scores, axis=0, keepdims=True))
             p = e * (1.0 / jnp.sum(e, axis=0, keepdims=True))
-            keep[2 * pair + i, :, aligned(g * 256, 256, 256)] = p
+            self.keep[2 * unit + i] = p
             probs.append(p)
-        probs = self.stack(*probs)
-        da_wide = self.spread(da[rows, aligned(g * 128, 128)])
-        self.own(dv, pair, g, nn(probs, da_wide))
-        self.across(at, pair, g, kvt[aligned(512 + g * 128, 128), rows], probs)
-
-    def backward(self, g, pair):
-        qkv, kvt, da, bias, mask, keep, dk, dv, dqt, at, gb = self.refs
+        self.wide[u] = self.stack(*probs)
+
+    def forward3(self, u, unit):
+        g, pair = self.place(unit)
         rows = aligned(pair * 128, 128)
-        da_wide = self.spread(da[rows, aligned(g * 128, 128)])
-        both = nt(self.diagonal(qkv[rows, aligned(1024 + g * 128, 128)]), da_wide)
+        probs = self.wide[u]
+        da_wide = self.spread(self.da[rows, aligned(g * 128, 128)])
+        self.own(self.dv, pair, g, nn(probs, da_wide))
+        self.across(self.at, pair, g, self.kvt[aligned(512 + g * 128, 128), rows], probs)
+
+    def backward1(self, u, unit):
+        g, pair = self.place(unit)
+        rows = aligned(pair * 128, 128)
+        da_wide = self.spread(self.da[rows, aligned(g * 128, 128)])
+        self.raw[u] = nt(self.diagonal(self.qkv[rows, aligned(1024 + g * 128, 128)]), da_wide)
+
+    def backward2(self, u, unit):
+        g, pair = self.place(unit)
         parts = []
         for i in range(2):
-            p = keep[2 * pair + i, :, aligned(g * 256, 256, 256)]
-            dp = both[i * SEG : i * SEG + TP]
-            ds = p * (dp - jnp.sum(p * dp, axis=0, keepdims=True))
-            parts.append(ds)
+            p = self.keep[2 * unit + i]
+            dp = self.raw[u, i * SEG : i * SEG + TP, :]
+            parts.append(p * (dp - jnp.sum(p * dp, axis=0, keepdims=True)))
         total = parts[0] + parts[1]
         for k in range(2):
             block = aligned((2 * g + k) * TP, TP, 8)
-            gb[block, :] = gb[block, :] + total[:, k * 128 : (k + 1) * 128]
-        wide = self.stack(parts[0] * SCALE, parts[1] * SCALE)
-        q_wide = self.spread(qkv[rows, aligned(g * 128, 128)])
-        self.own(dk, pair, g, nn(wide, q_wide))
-        self.across(dqt, pair, g, kvt[aligned(g * 128, 128), rows], wide)
-
-    def run(self, pass_, g):
+            self.gb[block, :] = self.gb[block, :] + total[:, k * 128 : (k + 1) * 128]
+        self.wide[u] = self.stack(parts[0] * SCALE, parts[1] * SCALE)
+
+    def backward3(self, u, unit):
+        g, pair = self.place(unit)
+        rows = aligned(pair * 128, 128)
+        wide = self.wide[u]
+        q_wide = self.spread(self.qkv[rows, aligned(g * 128, 128)])
+        self.own(self.dk, pair, g, nn(wide, q_wide))
+        self.across(self.dqt, pair, g, self.kvt[aligned(g * 128, 128), rows], wide)
+
+    def stages(self, stages, t, which):
+        for n in (2, 1, 0):
+            if n in which:
+                for u in range(UNITS):
+                    stages[n](u, (t - n) * UNITS + u)
+
+    def run(self, stages, lo, hi):
+        if lo == 0:
+            self.stages(stages, 0, (0,))
+            self.stages(stages, 1, (0, 1))
+        end = STEPS if hi == STEPS else hi + 2
+
         def one(t, carry):
-            for u in range(UNITS):
-                pass_(g, t * UNITS + u)
+            self.stages(stages, t, (0, 1, 2))
             return carry
 
-        lax.fori_loop(0, WIN // 2 // UNITS, one, 0)
+        lax.fori_loop(lo + 2, end, one, 0)
+        if hi == STEPS:
+            self.stages(stages, STEPS, (1, 2))
+            self.stages(stages, STEPS + 1, (2,))
 
 
 def table_gradient(gb, relt):
@@ -348,7 +383,7 @@
             self.start("t%d" % stage, self.tt.at[stage, 0], self.tr.at[first + count + n], dev)
 
 
-def kernel(scale, *refs):
+def kernel(*refs):
     refs = list(refs)
 
     def take(n):
@@ -357,11 +392,10 @@
         return out
 
     tok_hbm, cot_hbm, reg, rel, wqkv_hbm, wproj_hbm, tab_t = take(7)
-    mom_qkv, mom_proj, mom_tab = take(3)
     out_qkv, out_proj, out_tab = take(3)
     tok, cot, wqkv, wproj, fetched = take(5)
     xp, cp, qkv, kvt, da, xpt = take(6)
-    bias, mask, keep, dk, dv, dqt, at, gb, pad, tabp, relt = take(11)
+    bias, mask, keep, dk, dv, dqt, at, gb, pad, tabp, relt, raw, wide = take(13)
     ex = Exchange(*refs)
 
     fetches = []
@@ -380,7 +414,9 @@
     fetches[3].wait()
     project(wqkv, wproj, xp, cp, qkv, kvt, da, xpt)
 
-    att = Attention(qkv, kvt, da, bias, mask, keep, dk, dv, dqt, at, gb)
+    att = Attention(qkv, kvt, da, bias, mask, keep, dk, dv, dqt, at, gb, raw, wide)
+    forward = att.forward1, att.forward2, att.forward3
+    backward = att.backward1, att.backward2, att.backward3
 
     def v_chunk(c):
         ex.put(c, 0, nn(xpt[...], dv[:, c * 256 : (c + 1) * 256]))
@@ -396,30 +432,28 @@
         ex.put(4 + g, 128, nn(xpt[...], dk[:, g * 128 : (g + 1) * 128]))
         ex.cores(4 + g)
 
-    att.run(att.forward, 0)
-    att.run(att.forward, 1)
+    att.run(forward, 0, 2 * GROUP)
     ex.greeted()
     v_chunk(0)
-    att.run(att.forward, 2)
+    att.run(forward, 2 * GROUP, 4 * GROUP)
     ex.first(0)
-    att.run(att.forward, 3)
     v_chunk(1)
     proj_chunk(0)
     ex.first(1)
     proj_chunk(1)
     ex.first(2)
-    att.run(att.backward, 0)
+    att.run(backward, 0, GROUP)
     ex.first(3)
     qk_chunk(0)
-    att.run(att.backward, 1)
+    att.run(backward, GROUP, 2 * GROUP)
     ex.first(4)
     ex.second(0, 4)
     qk_chunk(1)
-    att.run(att.backward, 2)
+    att.run(backward, 2 * GROUP, 3 * GROUP)
     ex.first(5)
     ex.third(0, 4)
     qk_chunk(2)
-    att.run(att.backward, 3)
+    att.run(backward, 3 * GROUP, 4 * GROUP)
     ex.first(6)
     qk_chunk(3)
     ex.second(4, 6)
@@ -429,23 +463,23 @@
     ex.finish("t0")
     ex.table_axis(None, 1, 0, 1, own + ex.tr[0], ex.along_x)
     ex.third(4, 6)
+    ex.table_axis("t1", 2, 1, 3, ex.tt[1, 0], ex.along_y)
     ex.second(6, 8)
-    ex.table_axis("t1", 2, 1, 3, ex.tt[1, 0], ex.along_y)
+    ex.table_axis("t2", 3, 4, 3, ex.tt[2, 0], ex.along_z)
     ex.third(6, 8)
-    ex.table_axis("t2", 3, 4, 3, ex.tt[2, 0], ex.along_z)
 
     def finish(lo, hi):
         for c, mine in zip(range(lo, hi), ex.last(lo, hi)):
             for r in range(2):
                 for part in range(2):
-                    value = mine[r : r + 1, part * 128 : (part + 1) * 128] * scale
+                    value = mine[r : r + 1, part * 128 : (part + 1) * 128]
                     if 2 <= c < 4:
                         k = r * 4 + (c - 2) * 2 + part
-                        out_proj[k : k + 1, :] = 0.9 * mom_proj[k : k + 1, :] + value
+                        out_proj[k : k + 1, :] = value
                     else:
                         col = 8 + c * 2 + part if c < 2 else part * 4 + c - 4
                         k = r * 12 + col
-                        out_qkv[k : k + 1, :] = 0.9 * mom_qkv[k : k + 1, :] + value
+                        out_qkv[k : k + 1, :] = value
 
     finish(0, 4)
     finish(4, 6)
@@ -462,10 +496,13 @@
     even = table * (1.0 - core) + other * core
     odd = table * core + other * (1.0 - core)
     for k in range(8):
-        out_tab[2 * k : 2 * k + 1, :] = 0.9 * mom_tab[2 * k : 2 * k + 1, :] + even[k : k + 1, 0:169] * scale
-        out_tab[2 * k + 1 : 2 * k + 2, :] = (
-            0.9 * mom_tab[2 * k + 1 : 2 * k + 2, :] + odd[k : k + 1, 0:169] * scale
-        )
+        out_tab[2 * k : 2 * k + 1, :] = even[k : k + 1, 0:169]
+        out_tab[2 * k + 1 : 2 * k + 2, :] = odd[k : k + 1, 0:169]
+
+
+def apply_kernel(scale, *refs):
+    for total, momentum, out in zip(refs[0:3], refs[3:6], refs[6:9]):
+        out[...] = 0.9 * momentum[...] + total[...] * scale
 
 
 SCRATCH = [
@@ -482,7 +519,7 @@
     pltpu.VMEM((D, 1024), BF),
     pltpu.VMEM((4, TP, 256), F32),
     pltpu.VMEM((WIN, TP, 128), F32),
-    pltpu.VMEM((WIN, TP, 1024), F32),
+    pltpu.VMEM((4 * WIN, TP, 256), F32),
     pltpu.VMEM((1024, D), BF),
     pltpu.VMEM((1024, D), BF),
     pltpu.VMEM((D, 1024), BF),
@@ -491,6 +528,8 @@
     pltpu.VMEM((128, 128), F32),
     pltpu.VMEM((16, 256), F32),
     pltpu.VMEM((TP, 128), F32),
+    pltpu.VMEM((UNITS, 128, 256), F32),
+    pltpu.VMEM((UNITS, 128, 256), BF),
     pltpu.VMEM((CHUNKS, 2, 2, 4, 4, 8, CH), F32),
     pltpu.VMEM((CHUNKS, 2, 4, 4, 8, CH), F32),
     pltpu.VMEM((CHUNKS, 3, 4, 8, CH), F32),
@@ -508,18 +547,21 @@
 ]
 
 
-def step(scale, *operands):
+OUT = (
+    jax.ShapeDtypeStruct((24, 128), F32),
+    jax.ShapeDtypeStruct((8, 128), F32),
+    jax.ShapeDtypeStruct((16, 169), F32),
+)
+
+
+def step(*operands):
     vm = pl.BlockSpec(memory_space=pltpu.VMEM)
     hbm = pl.BlockSpec(memory_space=pl.ANY)
     return pl.pallas_call(
-        functools.partial(kernel, scale),
+        kernel,
         name="step",
-        out_shape=(
-            jax.ShapeDtypeStruct((24, 128), F32),
-            jax.ShapeDtypeStruct((8, 128), F32),
-            jax.ShapeDtypeStruct((16, 169), F32),
-        ),
-        in_specs=[hbm, hbm, vm, vm, hbm, hbm, vm, vm, vm, vm],
+        out_shape=OUT,
+        in_specs=[hbm, hbm, vm, vm, hbm, hbm, vm],
         out_specs=(vm, vm, vm),
         scratch_shapes=SCRATCH,
         compiler_params=pltpu.CompilerParams(
@@ -528,14 +570,26 @@
     )(*operands)
 
 
+def apply(scale, *operands):
+    vm = pl.BlockSpec(memory_space=pltpu.VMEM)
+    return pl.pallas_call(
+        functools.partial(apply_kernel, scale),
+        name="apply",
+        out_shape=OUT,
+        in_specs=[vm] * 6,
+        out_specs=(vm, vm, vm),
+        compiler_params=pltpu.CompilerParams(vmem_limit_bytes=60 * 2**20),
+    )(*operands)
+
+
 def body(tokens, cotangent, regions, rel_index, w_qkv, w_proj, bias_table, mom_qkv, mom_proj, mom_table):
     win, count, dim = tokens.shape
     devices = lax.axis_size(("gx", "gy", "gz"))
     tok = jnp.transpose(tokens, (1, 0, 2)).reshape(count * win, dim)
     cot = jnp.transpose(cotangent, (1, 0, 2)).reshape(count * win, dim)
-    out_qkv, out_proj, out_tab = step(
-        1.0 / (win * devices), tok, cot, regions, rel_index, w_qkv, w_proj, bias_table.T,
-        mom_qkv.reshape(24, 128), mom_proj.reshape(8, 128), mom_table.T,
+    sums = step(tok, cot, regions, rel_index, w_qkv, w_proj, bias_table.T)
+    out_qkv, out_proj, out_tab = apply(
+        1.0 / (win * devices), *sums, mom_qkv.reshape(24, 128), mom_proj.reshape(8, 128), mom_table.T
     )
     return out_qkv.reshape(-1), out_proj.reshape(-1), out_tab.T
 

time: 70.9 us -> 57.7 us (0.81)
  Pallas kernels: 66 us -> 56.9 us
  local copies, waits for them, and re-layouts: 3.9 us -> 0 us
    pallas_call x1 -> x2, Pallas kernels: 66 us -> 56.9 us  [the longest x1 55.5 us: step(): pl.pallas_call(kernel, name='step', out_shape=OUT, in_specs=[hbm, hbm, vm...]
    unnamed x3 -> x0, local copies, waits for them, and re-layouts: 3.9 us -> none
where the time goes in v1:
time: 57.7 us; the launch traced here: 57.5 us
  Pallas kernels  56.9 us (99%)
  between operations  0.64 us (1%)
    pallas_call x1, Pallas kernels, step(): pl.pallas_call(kernel, name='step', out_shape=OUT, in_specs=[hbm, hbm, vm...  55.5 us
    pallas_call x1, Pallas kernels, apply(): pl.pallas_call(functools.partial(apply_kernel, scale), name='apply', out_...  1.41 us

profile of v1, /device:TPU:1, one launch (start us, length us, event | category | flops | bytes accessed | tf_op | source)
XLA Modules:
  0.0 57.5 jit_solution(13302495951280457121)
XLA Ops:
  0.6 55.5 %step.1 = (f32[24,128]{1,0:T(8,128)}, f32[8,128]{1,0:T(8,128)}, f32[16,169]{1,0:T(8,128)}) custom-call(bf16[784,512]{1,0:T(8,128)(2,1)} %bitcast.13, bf16[784,512]{1,0:T(8,128)(2,1)} %bitcast.14, s32[16,49]{1,0:T(8,128)} %refs_2_.1, s32[49,49]{1,0:T(8,128)} %refs_3_.1, bf16[512,1536]{1,0:T(8,128)(2,1)} %refs_4_.1, bf16[512,512]{1,0:T(8,128)(2,1)} %refs_5_.1, ...), custom_call_target="tpu_custom_call" | custom-call | tf_op jit(solution)/shard_map/step/pallas_call | solution.py:560
  56.1 1.4 %apply.1 = (f32[24,128]{1,0:T(8,128)}, f32[8,128]{1,0:T(8,128)}, f32[16,169]{1,0:T(8,128)}) custom-call(f32[24,128]{1,0:T(8,128)} %get-tuple-element.9.refs_0_, f32[8,128]{1,0:T(8,128)} %get-tuple-element.10.refs_1_, f32[16,169]{1,0:T(8,128)} %get-tuple-element.11.refs_2_, f32[24,128]{1,0:T(8,128)} %bitcast.17, f32[8,128]{1,0:T(8,128)} %bitcast.18, ...), custom_call_target="tpu_custom_call" | custom-call | tf_op jit(solution)/shard_map/apply/pallas_call | solution.py:575

commit v2 on v1

--- a/solution.py
+++ b/solution.py
@@ -120,10 +120,10 @@
 
 
 class Attention:
-    def __init__(self, qkv, kvt, da, bias, mask, keep, dk, dv, dqt, at, gb, raw, wide):
+    def __init__(self, qkv, kvt, da, bias, mask, keep, dk, dv, dqt, at, gb, raw, wide, grads):
         self.qkv, self.kvt, self.da, self.bias, self.mask = qkv, kvt, da, bias, mask
         self.keep, self.dk, self.dv, self.dqt, self.at = keep, dk, dv, dqt, at
-        self.gb, self.raw, self.wide = gb, raw, wide
+        self.gb, self.raw, self.wide, self.grads = gb, raw, wide, grads
         lane = iota((SEG, 256), 1) % 128
         self.heads = [onehot(lane // HEAD_DIM == h) for h in range(4)]
         self.zero = jnp.zeros((SEG, 128), BF)
@@ -209,36 +209,40 @@
         for k in range(2):
             block = aligned((2 * g + k) * TP, TP, 8)
             self.gb[block, :] = self.gb[block, :] + total[:, k * 128 : (k + 1) * 128]
-        self.wide[u] = self.stack(parts[0] * SCALE, parts[1] * SCALE)
-
-    def backward3(self, u, unit):
+        self.grads[unit] = self.stack(parts[0] * SCALE, parts[1] * SCALE)
+
+    def backward_k(self, u, unit):
         g, pair = self.place(unit)
         rows = aligned(pair * 128, 128)
-        wide = self.wide[u]
         q_wide = self.spread(self.qkv[rows, aligned(g * 128, 128)])
-        self.own(self.dk, pair, g, nn(wide, q_wide))
-        self.across(self.dqt, pair, g, self.kvt[aligned(g * 128, 128), rows], wide)
+        self.own(self.dk, pair, g, nn(self.grads[unit], q_wide))
+
+    def backward_q(self, u, unit):
+        g, pair = self.place(unit)
+        rows = aligned(pair * 128, 128)
+        self.across(self.dqt, pair, g, self.kvt[aligned(g * 128, 128), rows], self.grads[unit])
 
     def stages(self, stages, t, which):
-        for n in (2, 1, 0):
-            if n in which:
-                for u in range(UNITS):
-                    stages[n](u, (t - n) * UNITS + u)
+        for n in reversed(which):
+            for u in range(UNITS):
+                stages[n](u, (t - n) * UNITS + u)
 
     def run(self, stages, lo, hi):
+        ahead = len(stages) - 1
+        whole = tuple(range(len(stages)))
         if lo == 0:
-            self.stages(stages, 0, (0,))
-            self.stages(stages, 1, (0, 1))
-        end = STEPS if hi == STEPS else hi + 2
+            for t in range(ahead):
+                self.stages(stages, t, whole[: t + 1])
+        end = STEPS if hi == STEPS else hi + ahead
 
         def one(t, carry):
-            self.stages(stages, t, (0, 1, 2))
+            self.stages(stages, t, whole)
             return carry
 
-        lax.fori_loop(lo + 2, end, one, 0)
+        lax.fori_loop(lo + ahead, end, one, 0)
         if hi == STEPS:
-            self.stages(stages, STEPS, (1, 2))
-            self.stages(stages, STEPS + 1, (2,))
+            for t in range(ahead):
+                self.stages(stages, STEPS + t, whole[t + 1 :])
 
 
 def table_gradient(gb, relt):
@@ -395,7 +399,7 @@
     out_qkv, out_proj, out_tab = take(3)
     tok, cot, wqkv, wproj, fetched = take(5)
     xp, cp, qkv, kvt, da, xpt = take(6)
-    bias, mask, keep, dk, dv, dqt, at, gb, pad, tabp, relt, raw, wide = take(13)
+    bias, mask, keep, dk, dv, dqt, at, gb, pad, tabp, relt, raw, wide, grads = take(14)
     ex = Exchange(*refs)
 
     fetches = []
@@ -414,9 +418,9 @@
     fetches[3].wait()
     project(wqkv, wproj, xp, cp, qkv, kvt, da, xpt)
 
-    att = Attention(qkv, kvt, da, bias, mask, keep, dk, dv, dqt, at, gb, raw, wide)
+    att = Attention(qkv, kvt, da, bias, mask, keep, dk, dv, dqt, at, gb, raw, wide, grads)
     forward = att.forward1, att.forward2, att.forward3
-    backward = att.backward1, att.backward2, att.backward3
+    backward = att.backward1, att.backward2
 
     def v_chunk(c):
         ex.put(c, 0, nn(xpt[...], dv[:, c * 256 : (c + 1) * 256]))
@@ -427,45 +431,51 @@
         ex.put(2 + c, 0, nn(at[...], y))
         ex.cores(2 + c)
 
-    def qk_chunk(g):
-        ex.put(4 + g, 0, nt(xpt[...], dqt[g * 128 : (g + 1) * 128, :]))
-        ex.put(4 + g, 128, nn(xpt[...], dk[:, g * 128 : (g + 1) * 128]))
-        ex.cores(4 + g)
-
-    att.run(forward, 0, 2 * GROUP)
+    def k_chunk(c):
+        ex.put(4 + 2 * c, 0, nn(xpt[...], dk[:, c * 256 : (c + 1) * 256]))
+        ex.cores(4 + 2 * c)
+
+    def q_chunk(c):
+        ex.put(5 + 2 * c, 0, nt(xpt[...], dqt[c * 256 : (c + 1) * 256, :]))
+        ex.cores(5 + 2 * c)
+
+    half = 2 * GROUP
+    att.run(forward, 0, half)
     ex.greeted()
     v_chunk(0)
-    att.run(forward, 2 * GROUP, 4 * GROUP)
+    att.run(forward, half, STEPS)
     ex.first(0)
     v_chunk(1)
     proj_chunk(0)
     ex.first(1)
     proj_chunk(1)
     ex.first(2)
-    att.run(backward, 0, GROUP)
+    att.run(backward, 0, half)
     ex.first(3)
-    qk_chunk(0)
-    att.run(backward, GROUP, 2 * GROUP)
+    att.run((att.backward_k,), 0, half)
+    k_chunk(0)
+    att.run((att.backward_q,), 0, half)
     ex.first(4)
+    q_chunk(0)
     ex.second(0, 4)
-    qk_chunk(1)
-    att.run(backward, 2 * GROUP, 3 * GROUP)
+    att.run(backward, half, STEPS)
     ex.first(5)
+    att.run((att.backward_k,), half, STEPS)
+    k_chunk(1)
+    ex.table_cores(table_gradient(gb, relt))
+    ex.first(6)
     ex.third(0, 4)
-    qk_chunk(2)
-    att.run(backward, 3 * GROUP, 4 * GROUP)
-    ex.first(6)
-    qk_chunk(3)
-    ex.second(4, 6)
-    ex.table_cores(table_gradient(gb, relt))
-    ex.first(7)
+    att.run((att.backward_q,), half, STEPS)
     own = ex.tt[0, ex.core]
     ex.finish("t0")
     ex.table_axis(None, 1, 0, 1, own + ex.tr[0], ex.along_x)
+    q_chunk(1)
+    ex.second(4, 6)
+    ex.table_axis("t1", 2, 1, 3, ex.tt[1, 0], ex.along_y)
+    ex.first(7)
     ex.third(4, 6)
-    ex.table_axis("t1", 2, 1, 3, ex.tt[1, 0], ex.along_y)
+    ex.table_axis("t2", 3, 4, 3, ex.tt[2, 0], ex.along_z)
     ex.second(6, 8)
-    ex.table_axis("t2", 3, 4, 3, ex.tt[2, 0], ex.along_z)
     ex.third(6, 8)
 
     def finish(lo, hi):
@@ -477,7 +487,7 @@
                         k = r * 4 + (c - 2) * 2 + part
                         out_proj[k : k + 1, :] = value
                     else:
-                        col = 8 + c * 2 + part if c < 2 else part * 4 + c - 4
+                        col = (8, 10, 0, 0, 4, 0, 6, 2)[c] + part
                         k = r * 12 + col
                         out_qkv[k : k + 1, :] = value
 
@@ -530,6 +540,7 @@
     pltpu.VMEM((TP, 128), F32),
     pltpu.VMEM((UNITS, 128, 256), F32),
     pltpu.VMEM((UNITS, 128, 256), BF),
+    pltpu.VMEM((2 * WIN, 128, 256), BF),
     pltpu.VMEM((CHUNKS, 2, 2, 4, 4, 8, CH), F32),
     pltpu.VMEM((CHUNKS, 2, 4, 4, 8, CH), F32),
     pltpu.VMEM((CHUNKS, 3, 4, 8, CH), F32),

time: 57.7 us -> 57 us (0.988)
  Pallas kernels: 56.9 us -> 56.2 us
    pallas_call x1, Pallas kernels: 55.5 us -> 54.8 us  [step(): pl.pallas_call(kernel, name='step', out_shape=OUT, in_specs=[hbm, hbm, vm...]
where the time goes in v2:
time: 57 us; the launch traced here: 56.8 us
  Pallas kernels  56.2 us (99%)
  between operations  0.64 us (1%)
    pallas_call x1, Pallas kernels, step(): pl.pallas_call(kernel, name='step', out_shape=OUT, in_specs=[hbm, hbm, vm...  54.8 us
    pallas_call x1, Pallas kernels, apply(): pl.pallas_call(functools.partial(apply_kernel, scale), name='apply', out_...  1.41 us

profile of v2, /device:TPU:1, one launch (start us, length us, event | category | flops | bytes accessed | tf_op | source)
XLA Modules:
  0.0 56.8 jit_solution(3795186445747764959)
XLA Ops:
  0.6 54.8 %step.1 = (f32[24,128]{1,0:T(8,128)}, f32[8,128]{1,0:T(8,128)}, f32[16,169]{1,0:T(8,128)}) custom-call(bf16[784,512]{1,0:T(8,128)(2,1)} %bitcast.13, bf16[784,512]{1,0:T(8,128)(2,1)} %bitcast.14, s32[16,49]{1,0:T(8,128)} %refs_2_.1, s32[49,49]{1,0:T(8,128)} %refs_3_.1, bf16[512,1536]{1,0:T(8,128)(2,1)} %refs_4_.1, bf16[512,512]{1,0:T(8,128)(2,1)} %refs_5_.1, ...), custom_call_target="tpu_custom_call" | custom-call | tf_op jit(solution)/shard_map/step/pallas_call | solution.py:571
  55.4 1.4 %apply.1 = (f32[24,128]{1,0:T(8,128)}, f32[8,128]{1,0:T(8,128)}, f32[16,169]{1,0:T(8,128)}) custom-call(f32[24,128]{1,0:T(8,128)} %get-tuple-element.9.refs_0_, f32[8,128]{1,0:T(8,128)} %get-tuple-element.10.refs_1_, f32[16,169]{1,0:T(8,128)} %get-tuple-element.11.refs_2_, f32[24,128]{1,0:T(8,128)} %bitcast.17, f32[8,128]{1,0:T(8,128)} %bitcast.18, ...), custom_call_target="tpu_custom_call" | custom-call | tf_op jit(solution)/shard_map/apply/pallas_call | solution.py:586

commit v3 on v2

--- a/solution.py
+++ b/solution.py
@@ -395,27 +395,33 @@
         del refs[:n]
         return out
 
-    tok_hbm, cot_hbm, reg, rel, wqkv_hbm, wproj_hbm, tab_t = take(7)
+    tok_hbm, cot_hbm, reg_hbm, rel_hbm, wqkv_hbm, wproj_hbm, tab_hbm = take(7)
     out_qkv, out_proj, out_tab = take(3)
-    tok, cot, wqkv, wproj, fetched = take(5)
+    rel, reg, tab_t, tok, cot, wqkv, wproj, fetched = take(8)
     xp, cp, qkv, kvt, da, xpt = take(6)
     bias, mask, keep, dk, dv, dqt, at, gb, pad, tabp, relt, raw, wide, grads = take(14)
     ex = Exchange(*refs)
 
     fetches = []
-    for n, (src, dst) in enumerate(((tok_hbm, tok), (cot_hbm, cot), (wqkv_hbm, wqkv), (wproj_hbm, wproj))):
+    moves = (
+        (rel_hbm, rel), (reg_hbm, reg), (tab_hbm, tab_t),
+        (tok_hbm, tok), (cot_hbm, cot), (wqkv_hbm, wqkv), (wproj_hbm, wproj),
+    )
+    for n, (src, dst) in enumerate(moves):
         fetch = pltpu.make_async_copy(src, dst, fetched.at[n])
         fetch.start()
         fetches.append(fetch)
     ex.greet()
+    for fetch in fetches[:3]:
+        fetch.wait()
     small_tables(reg, rel, tab_t, bias, mask, pad, tabp, relt)
     gb[...] = jnp.zeros_like(gb)
-    fetches[0].wait()
+    fetches[3].wait()
     gather_windows(tok, xp)
-    fetches[1].wait()
+    fetches[4].wait()
     gather_windows(cot, cp)
-    fetches[2].wait()
-    fetches[3].wait()
+    fetches[5].wait()
+    fetches[6].wait()
     project(wqkv, wproj, xp, cp, qkv, kvt, da, xpt)
 
     att = Attention(qkv, kvt, da, bias, mask, keep, dk, dv, dqt, at, gb, raw, wide, grads)
@@ -440,44 +446,6 @@
         ex.cores(5 + 2 * c)
 
     half = 2 * GROUP
-    att.run(forward, 0, half)
-    ex.greeted()
-    v_chunk(0)
-    att.run(forward, half, STEPS)
-    ex.first(0)
-    v_chunk(1)
-    proj_chunk(0)
-    ex.first(1)
-    proj_chunk(1)
-    ex.first(2)
-    att.run(backward, 0, half)
-    ex.first(3)
-    att.run((att.backward_k,), 0, half)
-    k_chunk(0)
-    att.run((att.backward_q,), 0, half)
-    ex.first(4)
-    q_chunk(0)
-    ex.second(0, 4)
-    att.run(backward, half, STEPS)
-    ex.first(5)
-    att.run((att.backward_k,), half, STEPS)
-    k_chunk(1)
-    ex.table_cores(table_gradient(gb, relt))
-    ex.first(6)
-    ex.third(0, 4)
-    att.run((att.backward_q,), half, STEPS)
-    own = ex.tt[0, ex.core]
-    ex.finish("t0")
-    ex.table_axis(None, 1, 0, 1, own + ex.tr[0], ex.along_x)
-    q_chunk(1)
-    ex.second(4, 6)
-    ex.table_axis("t1", 2, 1, 3, ex.tt[1, 0], ex.along_y)
-    ex.first(7)
-    ex.third(4, 6)
-    ex.table_axis("t2", 3, 4, 3, ex.tt[2, 0], ex.along_z)
-    ex.second(6, 8)
-    ex.third(6, 8)
-
     def finish(lo, hi):
         for c, mine in zip(range(lo, hi), ex.last(lo, hi)):
             for r in range(2):
@@ -491,7 +459,48 @@
                         k = r * 12 + col
                         out_qkv[k : k + 1, :] = value
 
+    quarter = GROUP
+    att.run(forward, 0, half)
+    ex.greeted()
+    v_chunk(0)
+    att.run(forward, half, STEPS)
+    ex.first(0)
+    v_chunk(1)
+    proj_chunk(0)
+    proj_chunk(1)
+    att.run(backward, 0, quarter)
+    ex.first(1)
+    ex.first(2)
+    att.run(backward, quarter, half)
+    ex.first(3)
+    att.run((att.backward_k,), 0, half)
+    k_chunk(0)
+    att.run((att.backward_q,), 0, half)
+    q_chunk(0)
+    att.run(backward, half, half + quarter)
+    ex.first(4)
+    att.run(backward, half + quarter, STEPS)
+    ex.first(5)
+    ex.second(0, 4)
+    att.run((att.backward_k,), half, STEPS)
+    k_chunk(1)
+    ex.table_cores(table_gradient(gb, relt))
+    att.run((att.backward_q,), half, half + quarter)
+    ex.first(6)
+    own = ex.tt[0, ex.core]
+    ex.finish("t0")
+    ex.table_axis(None, 1, 0, 1, own + ex.tr[0], ex.along_x)
+    ex.third(0, 4)
+    att.run((att.backward_q,), half + quarter, STEPS)
+    q_chunk(1)
+    ex.second(4, 6)
+    ex.first(7)
+    ex.table_axis("t1", 2, 1, 3, ex.tt[1, 0], ex.along_y)
+    ex.third(4, 6)
+    ex.second(6, 8)
+    ex.table_axis("t2", 3, 4, 3, ex.tt[2, 0], ex.along_z)
     finish(0, 4)
+    ex.third(6, 8)
     finish(4, 6)
     finish(6, 8)
     ex.finish("t3")
@@ -516,11 +525,14 @@
 
 
 SCRATCH = [
+    pltpu.VMEM((TOK, TOK), jnp.int32),
+    pltpu.VMEM((WIN, TOK), jnp.int32),
+    pltpu.VMEM((16, 169), F32),
     pltpu.VMEM((784, D), BF),
     pltpu.VMEM((784, D), BF),
     pltpu.VMEM((D, 3 * D), BF),
     pltpu.VMEM((D, D), BF),
-    pltpu.SemaphoreType.DMA((4,)),
+    pltpu.SemaphoreType.DMA((7,)),
     pltpu.VMEM((WIN, SEG, D), BF),
     pltpu.VMEM((WIN, SEG, D), BF),
     pltpu.VMEM((1024, 3 * D), BF),
@@ -572,7 +584,7 @@
         kernel,
         name="step",
         out_shape=OUT,
-        in_specs=[hbm, hbm, vm, vm, hbm, hbm, vm],
+        in_specs=[hbm] * 7,
         out_specs=(vm, vm, vm),
         scratch_shapes=SCRATCH,
         compiler_params=pltpu.CompilerParams(

time: 57 us -> 55.4 us (0.972)
  Pallas kernels: 56.2 us -> 54.7 us
    pallas_call x1, Pallas kernels: 54.8 us -> 53.2 us  [step(): pl.pallas_call(kernel, name='step', out_shape=OUT, in_specs=[hbm] * 7, ou...]
where the time goes in v3:
time: 55.4 us; the launch traced here: 55.3 us
  Pallas kernels  54.7 us (99%)
  between operations  0.64 us (1%)
    pallas_call x1, Pallas kernels, step(): pl.pallas_call(kernel, name='step', out_shape=OUT, in_specs=[hbm] * 7, ou...  53.2 us
    pallas_call x1, Pallas kernels, apply(): pl.pallas_call(functools.partial(apply_kernel, scale), name='apply', out_...  1.41 us

profile of v3, /device:TPU:1, one launch (start us, length us, event | category | flops | bytes accessed | tf_op | source)
XLA Modules:
  0.0 55.3 jit_solution(6003265576022663151)
XLA Ops:
  0.6 53.2 %step.1 = (f32[24,128]{1,0:T(8,128)}, f32[8,128]{1,0:T(8,128)}, f32[16,169]{1,0:T(8,128)}) custom-call(bf16[784,512]{1,0:T(8,128)(2,1)} %bitcast.13, bf16[784,512]{1,0:T(8,128)(2,1)} %bitcast.14, s32[16,49]{1,0:T(8,128)} %refs_2_.1, s32[49,49]{1,0:T(8,128)} %refs_3_.1, bf16[512,1536]{1,0:T(8,128)(2,1)} %refs_4_.1, bf16[512,512]{1,0:T(8,128)(2,1)} %refs_5_.1, ...), custom_call_target="tpu_custom_call" | custom-call | tf_op jit(solution)/shard_map/step/pallas_call | solution.py:583
  53.9 1.4 %apply.1 = (f32[24,128]{1,0:T(8,128)}, f32[8,128]{1,0:T(8,128)}, f32[16,169]{1,0:T(8,128)}) custom-call(f32[24,128]{1,0:T(8,128)} %get-tuple-element.9.refs_0_, f32[8,128]{1,0:T(8,128)} %get-tuple-element.10.refs_1_, f32[16,169]{1,0:T(8,128)} %get-tuple-element.11.refs_2_, f32[24,128]{1,0:T(8,128)} %bitcast.17, f32[8,128]{1,0:T(8,128)} %bitcast.18, ...), custom_call_target="tpu_custom_call" | custom-call | tf_op jit(solution)/shard_map/apply/pallas_call | solution.py:598

commit v4 on v3

--- a/solution.py
+++ b/solution.py
@@ -17,9 +17,9 @@
 D = 512
 HEAD_DIM = 32
 SCALE = HEAD_DIM ** -0.5
-UNITS = 4
-STEPS = 4 * WIN // 2 // UNITS
-GROUP = STEPS // 4
+UNITS = 8
+ALL = 4 * WIN // 2
+GROUP = ALL // 4
 CH = 256
 CHUNKS = 8
 
@@ -120,10 +120,10 @@
 
 
 class Attention:
-    def __init__(self, qkv, kvt, da, bias, mask, keep, dk, dv, dqt, at, gb, raw, wide, grads):
+    def __init__(self, qkv, kvt, da, bias, mask, keep, dk, dv, dqt, at, gb, wide, grads):
         self.qkv, self.kvt, self.da, self.bias, self.mask = qkv, kvt, da, bias, mask
         self.keep, self.dk, self.dv, self.dqt, self.at = keep, dk, dv, dqt, at
-        self.gb, self.raw, self.wide, self.grads = gb, raw, wide, grads
+        self.gb, self.wide, self.grads = gb, wide, grads
         lane = iota((SEG, 256), 1) % 128
         self.heads = [onehot(lane // HEAD_DIM == h) for h in range(4)]
         self.zero = jnp.zeros((SEG, 128), BF)
@@ -166,17 +166,14 @@
     def place(self, unit):
         return unit // (WIN // 2), unit % (WIN // 2)
 
-    def forward1(self, u, unit):
+    def forward12(self, u, unit):
         g, pair = self.place(unit)
         rows = aligned(pair * 128, 128)
         q_wide = self.spread(self.qkv[rows, aligned(g * 128, 128)])
-        self.raw[u] = nt(self.diagonal(self.qkv[rows, aligned(512 + g * 128, 128)]), q_wide)
-
-    def forward2(self, u, unit):
-        g, pair = self.place(unit)
+        raw = nt(self.diagonal(self.qkv[rows, aligned(512 + g * 128, 128)]), q_wide)
         probs = []
         for i in range(2):
-            scores = self.raw[u, i * SEG : i * SEG + TP, :] * SCALE + self.bias[g]
+            scores = raw[i * SEG : i * SEG + TP] * SCALE + self.bias[g]
             scores = scores + jnp.concatenate([self.mask[2 * pair + i]] * 2, axis=1)
             e = jnp.exp(scores - jnp.max(scores, axis=0, keepdims=True))
             p = e * (1.0 / jnp.sum(e, axis=0, keepdims=True))
@@ -192,18 +189,15 @@
         self.own(self.dv, pair, g, nn(probs, da_wide))
         self.across(self.at, pair, g, self.kvt[aligned(512 + g * 128, 128), rows], probs)
 
-    def backward1(self, u, unit):
+    def backward12(self, u, unit):
         g, pair = self.place(unit)
         rows = aligned(pair * 128, 128)
         da_wide = self.spread(self.da[rows, aligned(g * 128, 128)])
-        self.raw[u] = nt(self.diagonal(self.qkv[rows, aligned(1024 + g * 128, 128)]), da_wide)
-
-    def backward2(self, u, unit):
-        g, pair = self.place(unit)
+        raw = nt(self.diagonal(self.qkv[rows, aligned(1024 + g * 128, 128)]), da_wide)
         parts = []
         for i in range(2):
             p = self.keep[2 * unit + i]
-            dp = self.raw[u, i * SEG : i * SEG + TP, :]
+            dp = raw[i * SEG : i * SEG + TP]
             parts.append(p * (dp - jnp.sum(p * dp, axis=0, keepdims=True)))
         total = parts[0] + parts[1]
         for k in range(2):
@@ -222,27 +216,31 @@
         rows = aligned(pair * 128, 128)
         self.across(self.dqt, pair, g, self.kvt[aligned(g * 128, 128), rows], self.grads[unit])
 
-    def stages(self, stages, t, which):
+    def stages(self, stages, units, t, which):
         for n in reversed(which):
-            for u in range(UNITS):
-                stages[n](u, (t - n) * UNITS + u)
-
-    def run(self, stages, lo, hi):
+            for u in range(units):
+                stages[n](u, (t - n) * units + u)
+
+    def run(self, stages, units, lo, hi):
         ahead = len(stages) - 1
         whole = tuple(range(len(stages)))
+        lo, hi, steps = lo // units, hi // units, ALL // units
         if lo == 0:
             for t in range(ahead):
-                self.stages(stages, t, whole[: t + 1])
-        end = STEPS if hi == STEPS else hi + ahead
+                self.stages(stages, units, t, whole[: t + 1])
+        end = steps if hi == steps else hi + ahead
 
         def one(t, carry):
-            self.stages(stages, t, whole)
+            self.stages(stages, units, t, whole)
             return carry
 
-        lax.fori_loop(lo + ahead, end, one, 0)
-        if hi == STEPS:
+        if end - lo - ahead == 1:
+            one(lo + ahead, 0)
+        else:
+            lax.fori_loop(lo + ahead, end, one, 0)
+        if hi == steps:
             for t in range(ahead):
-                self.stages(stages, STEPS + t, whole[t + 1 :])
+                self.stages(stages, units, steps + t, whole[t + 1 :])
 
 
 def table_gradient(gb, relt):
@@ -399,7 +397,7 @@
     out_qkv, out_proj, out_tab = take(3)
     rel, reg, tab_t, tok, cot, wqkv, wproj, fetched = take(8)
     xp, cp, qkv, kvt, da, xpt = take(6)
-    bias, mask, keep, dk, dv, dqt, at, gb, pad, tabp, relt, raw, wide, grads = take(14)
+    bias, mask, keep, dk, dv, dqt, at, gb, pad, tabp, relt, wide, grads = take(13)
     ex = Exchange(*refs)
 
     fetches = []
@@ -424,9 +422,11 @@
     fetches[6].wait()
     project(wqkv, wproj, xp, cp, qkv, kvt, da, xpt)
 
-    att = Attention(qkv, kvt, da, bias, mask, keep, dk, dv, dqt, at, gb, raw, wide, grads)
-    forward = att.forward1, att.forward2, att.forward3
-    backward = att.backward1, att.backward2
+    att = Attention(qkv, kvt, da, bias, mask, keep, dk, dv, dqt, at, gb, wide, grads)
+    forward = (att.forward12, att.forward3), 4
+    backward = (att.backward12,), 8
+    to_keys = (att.backward_k,), 8
+    to_queries = (att.backward_q,), 8
 
     def v_chunk(c):
         ex.put(c, 0, nn(xpt[...], dv[:, c * 256 : (c + 1) * 256]))
@@ -460,49 +460,48 @@
                         out_qkv[k : k + 1, :] = value
 
     quarter = GROUP
-    att.run(forward, 0, half)
+    att.run(*forward, 0, half)
     ex.greeted()
     v_chunk(0)
-    att.run(forward, half, STEPS)
+    att.run(*forward, half, ALL)
     ex.first(0)
     v_chunk(1)
     proj_chunk(0)
     proj_chunk(1)
-    att.run(backward, 0, quarter)
+    att.run(*backward, 0, quarter)
     ex.first(1)
     ex.first(2)
-    att.run(backward, quarter, half)
+    att.run(*backward, quarter, half)
     ex.first(3)
-    att.run((att.backward_k,), 0, half)
+    att.run(*to_keys, 0, half)
     k_chunk(0)
-    att.run((att.backward_q,), 0, half)
+    att.run(*to_queries, 0, half)
     q_chunk(0)
-    att.run(backward, half, half + quarter)
+    att.run(*backward, half, half + quarter)
     ex.first(4)
-    att.run(backward, half + quarter, STEPS)
+    att.run(*backward, half + quarter, ALL)
     ex.first(5)
-    ex.second(0, 4)
-    att.run((att.backward_k,), half, STEPS)
-    k_chunk(1)
     ex.table_cores(table_gradient(gb, relt))
-    att.run((att.backward_q,), half, half + quarter)
-    ex.first(6)
+    ex.second(0, 3)
+    att.run(*to_keys, half, ALL)
     own = ex.tt[0, ex.core]
     ex.finish("t0")
     ex.table_axis(None, 1, 0, 1, own + ex.tr[0], ex.along_x)
-    ex.third(0, 4)
-    att.run((att.backward_q,), half + quarter, STEPS)
+    k_chunk(1)
+    att.run(*to_queries, half, half + quarter)
+    ex.first(6)
+    att.run(*to_queries, half + quarter, ALL)
+    ex.table_axis("t1", 2, 1, 3, ex.tt[1, 0], ex.along_y)
+    ex.third(0, 3)
     q_chunk(1)
-    ex.second(4, 6)
+    ex.second(3, 6)
     ex.first(7)
-    ex.table_axis("t1", 2, 1, 3, ex.tt[1, 0], ex.along_y)
-    ex.third(4, 6)
+    ex.table_axis("t2", 3, 4, 3, ex.tt[2, 0], ex.along_z)
+    ex.third(3, 6)
+    finish(0, 3)
     ex.second(6, 8)
-    ex.table_axis("t2", 3, 4, 3, ex.tt[2, 0], ex.along_z)
-    finish(0, 4)
     ex.third(6, 8)
-    finish(4, 6)
-    finish(6, 8)
+    finish(3, 6)
     ex.finish("t3")
     table = ex.tt[3, 0]
     for n in range(7):
@@ -510,6 +509,7 @@
     ex.tt[4, 0] = table
     ex.start("t4", ex.tt.at[4, 0], ex.tr.at[14], ex.partner)
     ex.finish("t4")
+    finish(6, 8)
     core = ex.core.astype(F32)
     other = ex.tr[14]
     even = table * (1.0 - core) + other * core
@@ -550,7 +550,6 @@
     pltpu.VMEM((128, 128), F32),
     pltpu.VMEM((16, 256), F32),
     pltpu.VMEM((TP, 128), F32),
-    pltpu.VMEM((UNITS, 128, 256), F32),
     pltpu.VMEM((UNITS, 128, 256), BF),
     pltpu.VMEM((2 * WIN, 128, 256), BF),
     pltpu.VMEM((CHUNKS, 2, 2, 4, 4, 8, CH), F32),

time: 55.4 us -> 51.2 us (0.924)
  Pallas kernels: 54.7 us -> 50.2 us
    pallas_call x1, Pallas kernels: 53.2 us -> 48.8 us  [step(): pl.pallas_call(kernel, name='step', out_shape=OUT, in_specs=[hbm] * 7, ou...]
where the time goes in v4:
time: 51.2 us; the launch traced here: 50.9 us
  Pallas kernels  50.2 us (98%)
  between operations  0.64 us (1%)
    pallas_call x1, Pallas kernels, step(): pl.pallas_call(kernel, name='step', out_shape=OUT, in_specs=[hbm] * 7, ou...  48.8 us
    pallas_call x1, Pallas kernels, apply(): pl.pallas_call(functools.partial(apply_kernel, scale), name='apply', out_...  1.41 us

profile of v4, /device:TPU:1, one launch (start us, length us, event | category | flops | bytes accessed | tf_op | source)
XLA Modules:
  0.0 50.9 jit_solution(7402119748222348125)
XLA Ops:
  0.6 48.8 %step.1 = (f32[24,128]{1,0:T(8,128)}, f32[8,128]{1,0:T(8,128)}, f32[16,169]{1,0:T(8,128)}) custom-call(bf16[784,512]{1,0:T(8,128)(2,1)} %bitcast.13, bf16[784,512]{1,0:T(8,128)(2,1)} %bitcast.14, s32[16,49]{1,0:T(8,128)} %refs_2_.1, s32[49,49]{1,0:T(8,128)} %refs_3_.1, bf16[512,1536]{1,0:T(8,128)(2,1)} %refs_4_.1, bf16[512,512]{1,0:T(8,128)(2,1)} %refs_5_.1, ...), custom_call_target="tpu_custom_call" | custom-call | tf_op jit(solution)/shard_map/step/pallas_call | solution.py:582
  49.5 1.4 %apply.1 = (f32[24,128]{1,0:T(8,128)}, f32[8,128]{1,0:T(8,128)}, f32[16,169]{1,0:T(8,128)}) custom-call(f32[24,128]{1,0:T(8,128)} %get-tuple-element.9.refs_0_, f32[8,128]{1,0:T(8,128)} %get-tuple-element.10.refs_1_, f32[16,169]{1,0:T(8,128)} %get-tuple-element.11.refs_2_, f32[24,128]{1,0:T(8,128)} %bitcast.17, f32[8,128]{1,0:T(8,128)} %bitcast.18, ...), custom_call_target="tpu_custom_call" | custom-call | tf_op jit(solution)/shard_map/apply/pallas_call | solution.py:597

commit v5 on v4

--- a/solution.py
+++ b/solution.py
@@ -20,6 +20,7 @@
 UNITS = 8
 ALL = 4 * WIN // 2
 GROUP = ALL // 4
+ENTRIES = 176
 CH = 256
 CHUNKS = 8
 
@@ -245,13 +246,13 @@
 
 def table_gradient(gb, relt):
     low = iota((8, 128), 1) < SEG
-    entry = iota((256, 128), 0).astype(F32)
-    total = jnp.zeros((32, 256), F32)
+    entry = iota((ENTRIES, 128), 0).astype(F32)
+    total = jnp.zeros((32, ENTRIES), F32)
 
     def line(j):
         if j >= TOK:
-            return jnp.zeros((32, 128), BF), jnp.zeros((256, 128), BF)
-        hot = onehot(entry == jnp.broadcast_to(relt[j : j + 1, :], (256, 128)))
+            return jnp.zeros((32, 128), BF), jnp.zeros((ENTRIES, 128), BF)
+        hot = onehot(entry == jnp.broadcast_to(relt[j : j + 1, :], (ENTRIES, 128)))
         pairs = gb[pl.ds(j, 8, stride=TP), :]
         split = jnp.concatenate([jnp.where(low, pairs, 0.0), jnp.where(low, 0.0, pairs)], axis=0)
         upper = split.astype(BF)
@@ -370,8 +371,9 @@
         return out
 
     def table_cores(self, value):
-        self.tt[0, 0] = value[0:8]
-        self.tt[0, 1] = value[8:16]
+        self.tt[0] = jnp.zeros_like(self.tt[0])
+        self.tt[0, 0, :, 0:ENTRIES] = value[0:8]
+        self.tt[0, 1, :, 0:ENTRIES] = value[8:16]
         self.start("t0", self.tt.at[0, 1 - self.core], self.tr.at[0], self.partner)
 
     def table_axis(self, key, stage, first, count, own, peers):
@@ -582,7 +584,7 @@
     return pl.pallas_call(
         kernel,
         name="step",
-        out_shape=OUT,
+        out_shape=tuple(pltpu.VMEM(o.shape, o.dtype) for o in OUT),
         in_specs=[hbm] * 7,
         out_specs=(vm, vm, vm),
         scratch_shapes=SCRATCH,
@@ -600,7 +602,7 @@
         out_shape=OUT,
         in_specs=[vm] * 6,
         out_specs=(vm, vm, vm),
-        compiler_params=pltpu.CompilerParams(vmem_limit_bytes=60 * 2**20),
+        compiler_params=pltpu.CompilerParams(vmem_limit_bytes=2 * 2**20),
     )(*operands)
 
 

time: 51.2 us -> 49.8 us (0.973)
  Pallas kernels: 50.2 us -> 48.8 us
    pallas_call x1, Pallas kernels: 1.41 us -> 0.62 us  [apply(): pl.pallas_call(functools.partial(apply_kernel, scale), name='apply', out_...]
    pallas_call x1, Pallas kernels: 48.8 us -> 48.2 us  [step(): pl.pallas_call(kernel, name='step', out_shape=tuple((pltpu.VMEM(o.shape,...]
where the time goes in v5:
time: 49.8 us; the launch traced here: 49.6 us
  Pallas kernels  48.8 us (98%)
  between operations  0.69 us (1%)
    pallas_call x1, Pallas kernels, step(): pl.pallas_call(kernel, name='step', out_shape=tuple((pltpu.VMEM(o.shape,...  48.2 us

profile of v5, /device:TPU:1, one launch (start us, length us, event | category | flops | bytes accessed | tf_op | source)
XLA Modules:
  0.0 49.6 jit_solution(1042641125414342967)
XLA Ops:
  0.6 0.0 copy-start
  0.6 0.0 copy-start.1
  0.7 0.0 copy-start.2
  0.7 48.2 %step.1 = (f32[24,128]{1,0:T(8,128)S(1)}, f32[8,128]{1,0:T(8,128)S(1)}, f32[16,169]{1,0:T(8,128)S(1)}) custom-call(bf16[784,512]{1,0:T(8,128)(2,1)} %bitcast.16, bf16[784,512]{1,0:T(8,128)(2,1)} %bitcast.17, s32[16,49]{1,0:T(8,128)} %refs_2_.1, s32[49,49]{1,0:T(8,128)} %refs_3_.1, bf16[512,1536]{1,0:T(8,128)(2,1)} %refs_4_.1, bf16[512,512]{1,0:T(8,128)(2,1)} %refs_5_.1, ...), custom_call_target="tpu_custom_call" | custom-call | tf_op jit(solution)/shard_map/step/pallas_call | solution.py:584
  48.9 0.0 copy-done
  48.9 0.0 copy-done.1
  48.9 0.0 copy-done.2
  48.9 0.6 %apply.1 = (f32[24,128]{1,0:T(8,128)}, f32[8,128]{1,0:T(8,128)}, f32[16,169]{1,0:T(8,128)}) custom-call(f32[24,128]{1,0:T(8,128)S(1)} %get-tuple-element.9.refs_0_, f32[8,128]{1,0:T(8,128)S(1)} %get-tuple-element.10.refs_1_, f32[16,169]{1,0:T(8,128)S(1)} %get-tuple-element.11.refs_2_, f32[24,128]{1,0:T(8,128)S(1)} %bitcast.14, f32[8,128]{1,0:T(8,128)S(1)} %bitcast.15, ...), custom_call_target="tpu_custom_call" | custom-call | tf_op jit(solution)/shard_map/apply/pallas_call | solution.py:599
Async XLA Ops:
  0.6 48.3 %copy-start = (f32[169,16]{0,1:T(8,128)S(1)}, f32[169,16]{0,1:T(8,128)}, u32[]{:S(2)}) copy-start(f32[169,16]{0,1:T(8,128)} %param.19) | copy-start | bytes 32452
  0.6 48.3 %copy-start.1 = (f32[3072]{0:T(1024)S(1)}, f32[3072]{0:T(1024)}, u32[]{:S(2)}) copy-start(f32[3072]{0:T(1024)} %param.17) | copy-start | bytes 36868
  0.7 48.3 %copy-start.2 = (f32[1024]{0:T(1024)S(1)}, f32[1024]{0:T(1024)}, u32[]{:S(2)}) copy-start(f32[1024]{0:T(1024)} %param.18) | copy-start | bytes 12292

commit v6 on v5

--- a/solution.py
+++ b/solution.py
@@ -404,21 +404,19 @@
 
     fetches = []
     moves = (
-        (rel_hbm, rel), (reg_hbm, reg), (tab_hbm, tab_t),
-        (tok_hbm, tok), (cot_hbm, cot), (wqkv_hbm, wqkv), (wproj_hbm, wproj),
+        (tok_hbm, tok), (rel_hbm, rel), (reg_hbm, reg), (tab_hbm, tab_t),
+        (cot_hbm, cot), (wqkv_hbm, wqkv), (wproj_hbm, wproj),
     )
     for n, (src, dst) in enumerate(moves):
         fetch = pltpu.make_async_copy(src, dst, fetched.at[n])
         fetch.start()
         fetches.append(fetch)
     ex.greet()
-    for fetch in fetches[:3]:
+    for fetch in fetches[:5]:
         fetch.wait()
+    gather_windows(tok, xp)
     small_tables(reg, rel, tab_t, bias, mask, pad, tabp, relt)
     gb[...] = jnp.zeros_like(gb)
-    fetches[3].wait()
-    gather_windows(tok, xp)
-    fetches[4].wait()
     gather_windows(cot, cp)
     fetches[5].wait()
     fetches[6].wait()
@@ -472,8 +470,8 @@
     proj_chunk(1)
     att.run(*backward, 0, quarter)
     ex.first(1)
+    att.run(*backward, quarter, half)
     ex.first(2)
-    att.run(*backward, quarter, half)
     ex.first(3)
     att.run(*to_keys, 0, half)
     k_chunk(0)
@@ -482,36 +480,38 @@
     att.run(*backward, half, half + quarter)
     ex.first(4)
     att.run(*backward, half + quarter, ALL)
+    ex.table_cores(table_gradient(gb, relt))
     ex.first(5)
-    ex.table_cores(table_gradient(gb, relt))
     ex.second(0, 3)
     att.run(*to_keys, half, ALL)
     own = ex.tt[0, ex.core]
     ex.finish("t0")
     ex.table_axis(None, 1, 0, 1, own + ex.tr[0], ex.along_x)
     k_chunk(1)
-    att.run(*to_queries, half, half + quarter)
+    att.run(*to_queries, half, ALL)
+    q_chunk(1)
     ex.first(6)
-    att.run(*to_queries, half + quarter, ALL)
+    ex.first(7)
     ex.table_axis("t1", 2, 1, 3, ex.tt[1, 0], ex.along_y)
+    ex.second(3, 6)
     ex.third(0, 3)
-    q_chunk(1)
-    ex.second(3, 6)
-    ex.first(7)
+    ex.second(6, 7)
     ex.table_axis("t2", 3, 4, 3, ex.tt[2, 0], ex.along_z)
+    ex.second(7, 8)
     ex.third(3, 6)
+    ex.third(6, 7)
+    ex.third(7, 8)
     finish(0, 3)
-    ex.second(6, 8)
-    ex.third(6, 8)
-    finish(3, 6)
     ex.finish("t3")
     table = ex.tt[3, 0]
     for n in range(7):
         table = table + ex.tr[7 + n]
     ex.tt[4, 0] = table
     ex.start("t4", ex.tt.at[4, 0], ex.tr.at[14], ex.partner)
+    finish(3, 6)
+    finish(6, 7)
     ex.finish("t4")
-    finish(6, 8)
+    finish(7, 8)
     core = ex.core.astype(F32)
     other = ex.tr[14]
     even = table * (1.0 - core) + other * core
@@ -566,8 +566,8 @@
     pltpu.VMEM((7, CHUNKS, 2, CH), F32),
     pltpu.VMEM((5, 2, 8, CH), F32),
     pltpu.VMEM((15, 8, CH), F32),
-    pltpu.SemaphoreType.DMA((120,)),
-    pltpu.SemaphoreType.DMA((120,)),
+    pltpu.SemaphoreType.DMA((128,)),
+    pltpu.SemaphoreType.DMA((128,)),
 ]
 
 

time: 49.8 us -> 47.9 us (0.962)
  Pallas kernels: 48.8 us -> 47.1 us
    pallas_call x1, Pallas kernels: 48.2 us -> 46.5 us  [step(): pl.pallas_call(kernel, name='step', out_shape=tuple((pltpu.VMEM(o.shape,...]
where the time goes in v6:
time: 47.9 us; the launch traced here: 47.8 us
  Pallas kernels  47.1 us (98%)
  between operations  0.69 us (1%)
    pallas_call x1, Pallas kernels, step(): pl.pallas_call(kernel, name='step', out_shape=tuple((pltpu.VMEM(o.shape,...  46.5 us

profile of v6, /device:TPU:1, one launch (start us, length us, event | category | flops | bytes accessed | tf_op | source)
XLA Modules:
  0.0 47.8 jit_solution(3089132014007345229)
XLA Ops:
  0.6 0.0 copy-start
  0.6 0.0 copy-start.1
  0.7 0.0 copy-start.2
  0.7 46.5 %step.1 = (f32[24,128]{1,0:T(8,128)S(1)}, f32[8,128]{1,0:T(8,128)S(1)}, f32[16,169]{1,0:T(8,128)S(1)}) custom-call(bf16[784,512]{1,0:T(8,128)(2,1)} %bitcast.16, bf16[784,512]{1,0:T(8,128)(2,1)} %bitcast.17, s32[16,49]{1,0:T(8,128)} %refs_2_.1, s32[49,49]{1,0:T(8,128)} %refs_3_.1, bf16[512,1536]{1,0:T(8,128)(2,1)} %refs_4_.1, bf16[512,512]{1,0:T(8,128)(2,1)} %refs_5_.1, ...), custom_call_target="tpu_custom_call" | custom-call | tf_op jit(solution)/shard_map/step/pallas_call | solution.py:584
  47.1 0.0 copy-done
  47.2 0.0 copy-done.1
  47.2 0.0 copy-done.2
  47.2 0.6 %apply.1 = (f32[24,128]{1,0:T(8,128)}, f32[8,128]{1,0:T(8,128)}, f32[16,169]{1,0:T(8,128)}) custom-call(f32[24,128]{1,0:T(8,128)S(1)} %get-tuple-element.9.refs_0_, f32[8,128]{1,0:T(8,128)S(1)} %get-tuple-element.10.refs_1_, f32[16,169]{1,0:T(8,128)S(1)} %get-tuple-element.11.refs_2_, f32[24,128]{1,0:T(8,128)S(1)} %bitcast.14, f32[8,128]{1,0:T(8,128)S(1)} %bitcast.15, ...), custom_call_target="tpu_custom_call" | custom-call | tf_op jit(solution)/shard_map/apply/pallas_call | solution.py:599
Async XLA Ops:
  0.6 46.5 %copy-start = (f32[169,16]{0,1:T(8,128)S(1)}, f32[169,16]{0,1:T(8,128)}, u32[]{:S(2)}) copy-start(f32[169,16]{0,1:T(8,128)} %param.19) | copy-start | bytes 32452
  0.6 46.5 %copy-start.1 = (f32[3072]{0:T(1024)S(1)}, f32[3072]{0:T(1024)}, u32[]{:S(2)}) copy-start(f32[3072]{0:T(1024)} %param.17) | copy-start | bytes 36868
  0.7 46.5 %copy-start.2 = (f32[1024]{0:T(1024)S(1)}, f32[1024]{0:T(1024)}, u32[]{:S(2)}) copy-start(f32[1024]{0:T(1024)} %param.18) | copy-start | bytes 12292

commit v7 on v6

--- a/solution.py
+++ b/solution.py
@@ -463,26 +463,27 @@
     att.run(*forward, 0, half)
     ex.greeted()
     v_chunk(0)
-    att.run(*forward, half, ALL)
+    att.run(*backward, 0, quarter)
+    att.run(*backward, quarter, half)
     ex.first(0)
-    v_chunk(1)
-    proj_chunk(0)
-    proj_chunk(1)
-    att.run(*backward, 0, quarter)
-    ex.first(1)
-    att.run(*backward, quarter, half)
-    ex.first(2)
-    ex.first(3)
     att.run(*to_keys, 0, half)
     k_chunk(0)
     att.run(*to_queries, 0, half)
     q_chunk(0)
+    ex.first(4)
+    att.run(*forward, half, ALL)
+    ex.first(5)
+    v_chunk(1)
+    proj_chunk(0)
+    proj_chunk(1)
     att.run(*backward, half, half + quarter)
-    ex.first(4)
+    ex.first(1)
+    ex.second(4, 6)
     att.run(*backward, half + quarter, ALL)
+    ex.first(2)
+    ex.first(3)
     ex.table_cores(table_gradient(gb, relt))
-    ex.first(5)
-    ex.second(0, 3)
+    ex.third(4, 6)
     att.run(*to_keys, half, ALL)
     own = ex.tt[0, ex.core]
     ex.finish("t0")
@@ -493,22 +494,21 @@
     ex.first(6)
     ex.first(7)
     ex.table_axis("t1", 2, 1, 3, ex.tt[1, 0], ex.along_y)
-    ex.second(3, 6)
-    ex.third(0, 3)
+    ex.second(0, 4)
     ex.second(6, 7)
     ex.table_axis("t2", 3, 4, 3, ex.tt[2, 0], ex.along_z)
     ex.second(7, 8)
-    ex.third(3, 6)
+    ex.third(0, 4)
     ex.third(6, 7)
     ex.third(7, 8)
-    finish(0, 3)
+    finish(4, 6)
     ex.finish("t3")
     table = ex.tt[3, 0]
     for n in range(7):
         table = table + ex.tr[7 + n]
     ex.tt[4, 0] = table
     ex.start("t4", ex.tt.at[4, 0], ex.tr.at[14], ex.partner)
-    finish(3, 6)
+    finish(0, 4)
     finish(6, 7)
     ex.finish("t4")
     finish(7, 8)

time: 47.9 us -> 51.9 us (1.084)
  Pallas kernels: 47.1 us -> 51.1 us
    pallas_call x1, Pallas kernels: 46.5 us -> 50.5 us  [step(): pl.pallas_call(kernel, name='step', out_shape=tuple((pltpu.VMEM(o.shape,...]
where the time goes in v7:
time: 51.9 us; the launch traced here: 51.8 us
  Pallas kernels  51.1 us (98%)
  between operations  0.69 us (1%)
    pallas_call x1, Pallas kernels, step(): pl.pallas_call(kernel, name='step', out_shape=tuple((pltpu.VMEM(o.shape,...  50.5 us

profile of v7, /device:TPU:1, one launch (start us, length us, event | category | flops | bytes accessed | tf_op | source)
XLA Modules:
  0.0 51.8 jit_solution(4992744699142221536)
XLA Ops:
  0.6 0.0 copy-start
  0.6 0.0 copy-start.1
  0.7 0.0 copy-start.2
  0.7 50.5 %step.1 = (f32[24,128]{1,0:T(8,128)S(1)}, f32[8,128]{1,0:T(8,128)S(1)}, f32[16,169]{1,0:T(8,128)S(1)}) custom-call(bf16[784,512]{1,0:T(8,128)(2,1)} %bitcast.16, bf16[784,512]{1,0:T(8,128)(2,1)} %bitcast.17, s32[16,49]{1,0:T(8,128)} %refs_2_.1, s32[49,49]{1,0:T(8,128)} %refs_3_.1, bf16[512,1536]{1,0:T(8,128)(2,1)} %refs_4_.1, bf16[512,512]{1,0:T(8,128)(2,1)} %refs_5_.1, ...), custom_call_target="tpu_custom_call" | custom-call | tf_op jit(solution)/shard_map/step/pallas_call | solution.py:584
  51.2 0.0 copy-done
  51.2 0.0 copy-done.1
  51.2 0.0 copy-done.2
  51.2 0.6 %apply.1 = (f32[24,128]{1,0:T(8,128)}, f32[8,128]{1,0:T(8,128)}, f32[16,169]{1,0:T(8,128)}) custom-call(f32[24,128]{1,0:T(8,128)S(1)} %get-tuple-element.9.refs_0_, f32[8,128]{1,0:T(8,128)S(1)} %get-tuple-element.10.refs_1_, f32[16,169]{1,0:T(8,128)S(1)} %get-tuple-element.11.refs_2_, f32[24,128]{1,0:T(8,128)S(1)} %bitcast.14, f32[8,128]{1,0:T(8,128)S(1)} %bitcast.15, ...), custom_call_target="tpu_custom_call" | custom-call | tf_op jit(solution)/shard_map/apply/pallas_call | solution.py:599
Async XLA Ops:
  0.6 50.6 %copy-start = (f32[169,16]{0,1:T(8,128)S(1)}, f32[169,16]{0,1:T(8,128)}, u32[]{:S(2)}) copy-start(f32[169,16]{0,1:T(8,128)} %param.19) | copy-start | bytes 32452
  0.6 50.6 %copy-start.1 = (f32[3072]{0:T(1024)S(1)}, f32[3072]{0:T(1024)}, u32[]{:S(2)}) copy-start(f32[3072]{0:T(1024)} %param.17) | copy-start | bytes 36868
  0.7 50.6 %copy-start.2 = (f32[1024]{0:T(1024)S(1)}, f32[1024]{0:T(1024)}, u32[]{:S(2)}) copy-start(f32[1024]{0:T(1024)} %param.18) | copy-start | bytes 12292
